TPU v7x, 32 devices: a whole 2x2x4 slice. The times are simulated.
32 devices in a mesh: band: 8 (over z, x), slab: 4 (over y, core).
Axes of the slice: x: 2, y: 2, z: 4, core: 2. Of those that a mesh axis runs over, the one named last changes fastest.
Arguments:
- orbitals: float32 [512, 64, 512], P('band', 'slab'), may hold values from -6 to 6
- potential: float32 [64, 512], P('slab'), may hold values from 0 to 1
- projectors: float32 [4, 2048, 128], replicated, may hold values from -0.125 to 0.125
- atom_kind: int32 [32], P('slab'), may hold values from 0 to 3
- atom_plane: int32 [32], P('slab'), may hold values from 0 to 60, as said below
- atom_coef: float32 [32, 128], P('slab'), may hold values from 0.2 to 1
- filter_cut: float32 [1], replicated, may hold values from 0.5 to 2
- filter_top: float32 [1], replicated, may hold values from 9 to 14
Outputs:
- new_orbitals: float32 [512, 32768], P(None, ('slab', 'band'))
Inputs may be any that keep to these rules, and one draw needn't show every extreme that they name: `atom_plane`: block i's 4 planes lie inside the slab of planes (i // 8) * 16 to (i // 8 + 1) * 16 - 1; blocks may share planes.
All inputs are finite; a program needn't handle non-finite values.
Results may differ from a plain program's by a relative error of at most 0.0003.
Values sent between devices are 32-bit elements; how exact they have to be, the bound alone decides.
A program may use at most 128 MiB of HBM per device.

v0:
```python
import jax
import jax.numpy as jnp
from jax import lax
from jax.sharding import PartitionSpec as P

GZ = 32
ORDER = 6
low_edge = -1.0
near_coef = 4.0 / 3.0
far_coef = -1.0 / 12.0
self_coef = -2.5
highest = lax.Precision.HIGHEST


def padded_2(value, sides, width):
    for axis, dim in sides:
        size, length = (lax.axis_size(axis), value.shape[dim])
        up = [(i, (i + 1) % size) for i in range(size)]
        down = [(j, i) for i, j in up]
        last = lax.slice_in_dim(value, length - width, length, axis=dim)
        first = lax.slice_in_dim(value, 0, width, axis=dim)
        before = lax.ppermute(last, axis, up)
        after = lax.ppermute(first, axis, down)
        value = jnp.concatenate([before, value, after], axis=dim)
    return value


def shifted(source, offset):
    if offset > 0:
        zeros_part = jnp.zeros(source.shape[:-1] + (offset,), source.dtype)
        return jnp.concatenate([zeros_part, source[..., :-offset]], axis=-1)
    zeros_part = jnp.zeros(source.shape[:-1] + (-offset,), source.dtype)
    return jnp.concatenate([source[..., -offset:], zeros_part], axis=-1)


def transverse(source, width_z):
    length_last = source.shape[-1]
    z_position = jnp.arange(length_last) % width_z
    result_sum = 2.0 * self_coef * source
    for offset, weight_coef in ((1, near_coef), (-1, near_coef), (2, far_coef), (-2, far_coef)):
        result_sum = result_sum + weight_coef * shifted(source, offset * width_z)
        inside = (z_position - offset >= 0) & (z_position - offset < width_z)
        result_sum = result_sum + weight_coef * jnp.where(inside, shifted(source, offset), 0.0)
    return result_sum


def local(
    orbitals, potential, projectors, atom_kind, atom_plane, atom_coef, filter_cut, filter_top
):
    band_count, planes, points = orbitals.shape
    kind_count, block_pts, func_count = projectors.shape
    atom_count = atom_kind.shape[0]
    block_depth = block_pts // points
    local_plane = atom_plane - lax.axis_index("slab") * planes
    plane_ids = jnp.arange(planes)
    depth_ids = jnp.arange(block_depth)
    selector = (
        plane_ids[None, None, :] == local_plane[:, None, None] + depth_ids[None, :, None]
    ).astype(jnp.float32)
    atom_tables = jnp.take(projectors, atom_kind, axis=0)
    coef_rows = atom_coef[:, None, :]

    def hamiltonian_fn(source):
        padded = padded_2(source, (("slab", 1),), 2)
        along_x = self_coef * source
        along_x = along_x + near_coef * (padded[:, 1 : planes + 1] + padded[:, 3 : planes + 3])
        along_x = along_x + far_coef * (padded[:, 0:planes] + padded[:, 4 : planes + 4])
        laplace = along_x + transverse(source, GZ)
        blocks = jnp.einsum("ajx,nxp->anjp", selector, source, precision=highest)
        blocks = blocks.reshape(atom_count, band_count, block_pts)
        coupled = jnp.einsum("anq,aqf->anf", blocks, atom_tables, precision=highest) * coef_rows
        spread_back = jnp.einsum("anf,aqf->anq", coupled, atom_tables, precision=highest)
        spread_back = spread_back.reshape(atom_count, band_count, block_depth, points)
        nonlocal_part = jnp.einsum("ajx,anjp->nxp", selector, spread_back, precision=highest)
        return -0.5 * laplace + potential[None] * source + nonlocal_part

    cut_value = filter_cut[0]
    top_value = filter_top[0]
    half_width = (top_value - cut_value) / 2.0
    centre = (top_value + cut_value) / 2.0
    sigma_now = half_width / (low_edge - centre)
    tau_value = 2.0 / sigma_now
    previous = orbitals
    current = (hamiltonian_fn(previous) - centre * previous) * (sigma_now / half_width)
    for step_index in range(ORDER - 1):
        sigma_next = 1.0 / (tau_value - sigma_now)
        upcoming = (hamiltonian_fn(current) - centre * current) * (
            2.0 * sigma_next / half_width
        ) - sigma_now * sigma_next * previous
        previous = current
        current = upcoming
        sigma_now = sigma_next
    flat_orbitals = current.reshape(band_count, planes * points)
    grid_layout = lax.all_to_all(flat_orbitals, "band", split_axis=1, concat_axis=0, tiled=True)
    point_total = grid_layout.shape[1] * lax.axis_size(("band", "slab"))
    partial_gram = jnp.dot(grid_layout, grid_layout.T, precision=highest) / point_total
    gram_matrix = lax.psum(partial_gram, ("band", "slab"))
    factor = jnp.linalg.cholesky(gram_matrix)
    return jax.scipy.linalg.solve_triangular(factor, grid_layout, lower=True)


def solution(mesh):
    in_specs = (
        P("band", "slab", None),
        P("slab", None),
        P(),
        P("slab"),
        P("slab"),
        P("slab", None),
        P(),
        P(),
    )
    out_specs = P(None, ("slab", "band"))
    return jax.shard_map(local, mesh=mesh, in_specs=in_specs, out_specs=out_specs, check_vma=False)
```

profile of v0, /device:TPU:0, one launch (start us, length us, event | category | flops | bytes accessed | tf_op | source)
XLA Modules:
  0.0 782.5 jit_solution(11253992471097181108)
XLA Ops:
  51.0 10.4 %convolution_multiply_fusion.6 = f32[8,64,128]{2,1,0:T(8,128)S(1)} fusion(f32[8,64,2048]{2,1,0:T(8,128)} %reshape.122, f32[8,128]{1,0:T(8,128)S(1)} %copy-done.24, f32[8,2048,128]{2,1,0:T(8,128)} %gather_fusion, pred[8]{0:T(512)(128)(4,1)S(1)} %compare_and_fusion), kind=kOutput, calls=%fused_computation.154 | convolution fusion | flops 1612775424 | bytes 12849160 | tf_op jit(solution)/shard_map/anq,aqf->anf/dot_general | solution.py:71
  61.5 10.5 %fusion.153 = f32[8,64,2048]{2,1,0:T(8,128)} fusion(f32[8,64,128]{2,1,0:T(8,128)S(1)} %convolution_multiply_fusion.6, f32[8,2048,128]{2,1,0:T(8,128)S(1)} %copy-done, pred[8]{0:T(512)(128)(4,1)S(1)} %compare_and_fusion), kind=kOutput, calls=%fused_computation.243 | convolution fusion | flops 1612709888 | bytes 12845064 | tf_op jit(solution)/shard_map/anf,aqf->anq/dot_general | solution.py:72
  81.7 12.0 %fusion.75 = f32[64,16,512]{2,1,0:T(8,128)S(1)} fusion(f32[64,2,512]{2,1,0:T(2,128)S(1)} %collective-permute-done, f32[64,16,512]{2,1,0:T(8,128)S(1)} %copy-done.1, f32[64,18,512]{2,1,0:T(8,128)} %copy-done.23, f32[64,16,510]{2,1,0:T(8,128)} %get-tuple-element.84, f32[64,16,448]{2,1,0:T(8,128)} %get-tuple-element.82, ...), kind=kOutput, calls=%fused_computation.107 | convolution fusion | flops 221249536 | bytes 28846600 | tf_op jit(solution)/shard_map/ajx,anjp->nxp/dot_general | solution.py:74
  115.4 9.3 %convolution_multiply_fusion.5 = f32[8,64,128]{2,1,0:T(8,128)S(1)} fusion(f32[8,64,2048]{2,1,0:T(8,128)} %reshape.124, f32[8,128]{1,0:T(8,128)S(1)} %copy-done.24, f32[8,2048,128]{2,1,0:T(8,128)} %gather_fusion, pred[8]{0:T(512)(128)(4,1)S(1)} %compare_and_fusion), kind=kOutput, calls=%fused_computation.153 | convolution fusion | flops 1612775424 | bytes 12849160 | tf_op jit(solution)/shard_map/anq,aqf->anf/dot_general | solution.py:71
  124.7 12.7 %fusion.152 = f32[8,64,2048]{2,1,0:T(8,128)} fusion(f32[8,64,128]{2,1,0:T(8,128)S(1)} %convolution_multiply_fusion.5, f32[8,2048,128]{2,1,0:T(8,128)} %gather_fusion, pred[8]{0:T(512)(128)(4,1)S(1)} %compare_and_fusion), kind=kOutput, calls=%fused_computation.242 | convolution fusion | flops 1612709888 | bytes 12845064 | tf_op jit(solution)/shard_map/anf,aqf->anq/dot_general | solution.py:72
  150.8 12.0 %fusion.63 = f32[64,16,512]{2,1,0:T(8,128)S(1)} fusion(f32[64,16,512]{2,1,0:T(8,128)S(1)} %copy-done.9, f32[64,2,512]{2,1,0:T(2,128)S(1)} %collective-permute-done.3, f32[64,2,512]{2,1,0:T(2,128)S(1)} %collective-permute-done.2, f32[64,16,512]{2,1,0:T(8,128)S(1)} %copy-done.1, f32[64,16,510]{2,1,0:T(8,128)} %get-tuple-element.74, ...), kind=kOutput, calls=%fused_computation.95 | convolution fusion | flops 223346688 | bytes 27011596 | tf_op jit(solution)/shard_map/ajx,anjp->nxp/dot_general | solution.py:74
  193.7 12.7 %fusion.151 = f32[8,64,2048]{2,1,0:T(8,128)} fusion(f32[8,64,128]{2,1,0:T(8,128)S(1)} %convolution_multiply_fusion.4, f32[8,2048,128]{2,1,0:T(8,128)} %gather_fusion, pred[8]{0:T(512)(128)(4,1)S(1)} %compare_and_fusion), kind=kOutput, calls=%fused_computation.241 | convolution fusion | flops 1612709888 | bytes 12845064 | tf_op jit(solution)/shard_map/anf,aqf->anq/dot_general | solution.py:72
  220.0 12.3 %fusion.50 = f32[64,16,512]{2,1,0:T(8,128)S(1)} fusion(f32[64,16,512]{2,1,0:T(8,128)S(1)} %copy-done.6, f32[64,2,512]{2,1,0:T(2,128)S(1)} %collective-permute-done.5, f32[64,2,512]{2,1,0:T(2,128)S(1)} %collective-permute-done.4, f32[64,16,512]{2,1,0:T(8,128)S(1)} %copy-done.10, f32[64,16,510]{2,1,0:T(8,128)} %get-tuple-element.64, ...), kind=kOutput, calls=%fused_computation.82 | convolution fusion | flops 223346688 | bytes 27011596 | tf_op jit(solution)/shard_map/ajx,anjp->nxp/dot_general | solution.py:74
  263.0 12.7 %fusion.150 = f32[8,64,2048]{2,1,0:T(8,128)} fusion(f32[8,64,128]{2,1,0:T(8,128)S(1)} %convolution_multiply_fusion.3, f32[8,2048,128]{2,1,0:T(8,128)} %gather_fusion, pred[8]{0:T(512)(128)(4,1)S(1)} %compare_and_fusion), kind=kOutput, calls=%fused_computation.240 | convolution fusion | flops 1612709888 | bytes 12845064 | tf_op jit(solution)/shard_map/anf,aqf->anq/dot_general | solution.py:72
  289.2 13.8 %fusion.37 = f32[64,16,512]{2,1,0:T(8,128)S(1)} fusion(f32[64,16,512]{2,1,0:T(8,128)} %copy-done.2, f32[64,2,512]{2,1,0:T(2,128)S(1)} %collective-permute-done.7, f32[64,2,512]{2,1,0:T(2,128)S(1)} %collective-permute-done.6, f32[64,16,512]{2,1,0:T(8,128)S(1)} %copy-done.7, f32[64,16,510]{2,1,0:T(8,128)} %get-tuple-element.54, ...), kind=kOutput, calls=%fused_computation.69 | convolution fusion | flops 223346688 | bytes 27011596 | tf_op jit(solution)/shard_map/ajx,anjp->nxp/dot_general | solution.py:74
  333.8 12.7 %fusion.149 = f32[8,64,2048]{2,1,0:T(8,128)} fusion(f32[8,64,128]{2,1,0:T(8,128)S(1)} %convolution_multiply_fusion.2, f32[8,2048,128]{2,1,0:T(8,128)} %gather_fusion, pred[8]{0:T(512)(128)(4,1)S(1)} %compare_and_fusion), kind=kOutput, calls=%fused_computation.239 | convolution fusion | flops 1612709888 | bytes 12845064 | tf_op jit(solution)/shard_map/anf,aqf->anq/dot_general | solution.py:72
  359.9 12.0 %fusion.24 = f32[64,16,512]{2,1,0:T(8,128)S(1)} fusion(f32[64,16,512]{2,1,0:T(8,128)S(1)} %fusion.37, f32[64,2,512]{2,1,0:T(2,128)S(1)} %collective-permute-done.9, f32[64,2,512]{2,1,0:T(2,128)S(1)} %collective-permute-done.8, f32[64,16,512]{2,1,0:T(8,128)S(1)} %copy-done.3, f32[64,16,510]{2,1,0:T(8,128)} %get-tuple-element.44, ...), kind=kOutput, calls=%fused_computation.56 | convolution fusion | flops 223346688 | bytes 27011596 | tf_op jit(solution)/shard_map/ajx,anjp->nxp/dot_general | solution.py:74
  402.8 12.8 %fusion.148 = f32[8,64,2048]{2,1,0:T(8,128)} fusion(f32[8,64,128]{2,1,0:T(8,128)S(1)} %convolution_multiply_fusion.1, f32[8,2048,128]{2,1,0:T(8,128)} %gather_fusion, pred[8]{0:T(512)(128)(4,1)S(1)} %compare_and_fusion), kind=kOutput, calls=%fused_computation.238 | convolution fusion | flops 1612709888 | bytes 12845064 | tf_op jit(solution)/shard_map/anf,aqf->anq/dot_general | solution.py:72
  428.9 12.5 %fusion.11 = f32[64,16,512]{2,1,0:T(8,128)} fusion(f32[64,16,512]{2,1,0:T(8,128)S(1)} %copy-done.12, f32[64,2,512]{2,1,0:T(2,128)S(1)} %collective-permute-done.11, f32[64,2,512]{2,1,0:T(2,128)S(1)} %collective-permute-done.10, f32[64,16,512]{2,1,0:T(8,128)S(1)} %fusion.37, f32[64,16,510]{2,1,0:T(8,128)} %get-tuple-element.34, ...), kind=kOutput, calls=%fused_computation.43 | convolution fusion | flops 223346688 | bytes 27011596 | tf_op jit(solution)/shard_map/ajx,anjp->nxp/dot_general | solution.py:74
  444.5 55.2 %all_to_all.19 = f32[64,8,1024]{2,0,1:T(8,128)S(1)} all-to-all(f32[64,8,1024]{2,0,1:T(8,128)S(1)} %copy.29), channel_id=1, replica_groups=mesh['band'=8,'slab'=4] {'band'}, dimensions={1} | all-to-all | bytes 4194304 | tf_op jit(solution)/shard_map/all_to_all | solution.py:94
  505.5 128.1 %all-reduce.51.cloned.1.call-done = f32[512,512]{0,1:T(8,128)} async-done(((f32[512,512]{0,1:T(8,128)}), f32[512,512]{0,1:T(8,128)}) %all-reduce.51.cloned.1.call-update) | async-done | bytes 1048592 | tf_op jit(solution)/shard_map/psum | solution.py:97
  635.5 11.7 %cholesky.104 = f32[128,128]{1,0:T(8,128)S(1)} custom-call(f32[128,128]{1,0:T(8,128)S(1)} %cholesky.266), custom_call_target="Cholesky" | custom-call | tf_op jit(solution)/shard_map/jit(cholesky)/cholesky | solution.py:98
  647.4 9.8 %custom-call.31 = f32[1,128,128]{1,2,0:T(8,128)S(1)} custom-call(f32[1,128,128]{2,1,0:T(8,128)S(1)} %get-tuple-element.96), custom_call_target="InvertDiagBlocksLowerTriangular" | custom-call | tf_op jit(solution)/shard_map/jit(cholesky)/cholesky | solution.py:98
  657.9 11.9 %cholesky.217 = f32[128,128]{1,0:T(8,128)S(1)} custom-call(f32[128,128]{1,0:T(8,128)S(1)} %cholesky.270), custom_call_target="Cholesky" | custom-call | tf_op jit(solution)/shard_map/jit(cholesky)/cholesky | solution.py:98
  671.2 9.8 %custom-call.32 = f32[1,128,128]{1,2,0:T(8,128)S(1)} custom-call(f32[1,128,128]{2,1,0:T(8,128)S(1)} %get-tuple-element.93), custom_call_target="InvertDiagBlocksLowerTriangular" | custom-call | tf_op jit(solution)/shard_map/jit(cholesky)/cholesky | solution.py:98
  681.7 11.7 %cholesky.238 = f32[128,128]{1,0:T(8,128)S(1)} custom-call(f32[128,128]{1,0:T(8,128)S(1)} %cholesky.275), custom_call_target="Cholesky" | custom-call | tf_op jit(solution)/shard_map/jit(cholesky)/cholesky | solution.py:98
  694.1 9.8 %custom-call.33 = f32[1,128,128]{1,2,0:T(8,128)S(1)} custom-call(f32[1,128,128]{2,1,0:T(8,128)S(1)} %get-tuple-element.90), custom_call_target="InvertDiagBlocksLowerTriangular" | custom-call | tf_op jit(solution)/shard_map/jit(cholesky)/cholesky | solution.py:98
  704.5 11.9 %cholesky.255 = f32[128,128]{1,0:T(8,128)S(1)} custom-call(f32[128,128]{1,0:T(8,128)S(1)} %convolution_subtract_fusion.4), custom_call_target="Cholesky" | custom-call | tf_op jit(solution)/shard_map/jit(cholesky)/cholesky | solution.py:98
  728.3 39.3 %custom-call.34 = f32[4,128,128]{1,2,0:T(8,128)S(1)} custom-call(f32[4,128,128]{2,1,0:T(8,128)S(1)} %get-tuple-element.12), custom_call_target="InvertDiagBlocksLowerTriangular" | custom-call | tf_op jit(solution)/shard_map/jit(_solve_triangular)/triangular_solve | solution.py:99
  (196 shorter events, 304.2 us)
Async XLA Ops:
  6.5 627.1 %all-reduce.51.cloned.1.call-start = ((), (), s32[]{:S(2)}) async-start(), calls=%async_computation.1 | async-start | bytes 2097152 | tf_op jit(solution)/shard_map/psum | solution.py:97
  8.3 70.2 %collective-permute-start.1 = (f32[64,2,512]{2,1,0:T(2,128)S(1)}, f32[64,2,512]{2,1,0:T(2,128)S(1)}, u32[]{:S(2)}, u32[]{:S(2)}) collective-permute-start(f32[64,2,512]{2,1,0:T(2,128)S(1)} %get-tuple-element.85), channel_id=1, source_target_pairs={{1,0},{2,1},{3,2},{0,3},{5,4},{6,5},{7,6},{4,7},{9,8},{10,9},{11,1... | collective-permute-start | bytes 786440 | tf_op jit(solution)/shard_map/ppermute | solution.py:23
  10.8 67.9 %collective-permute-start = (f32[64,2,512]{2,1,0:T(2,128)S(1)}, f32[64,2,512]{2,1,0:T(2,128)S(1)}, u32[]{:S(2)}, u32[]{:S(2)}) collective-permute-start(f32[64,2,512]{2,1,0:T(2,128)S(1)} %get-tuple-element.86), channel_id=1, source_target_pairs={{0,1},{1,2},{2,3},{3,0},{4,5},{5,6},{6,7},{7,4},{8,9},{9,10},{10,1... | collective-permute-start | bytes 786440 | tf_op jit(solution)/shard_map/ppermute | solution.py:22
  44.4 6.6 copy-start.24
  51.0 10.4 %copy-start = (f32[8,2048,128]{2,1,0:T(8,128)S(1)}, f32[8,2048,128]{2,1,0:T(8,128)}, u32[]{:S(2)}) copy-start(f32[8,2048,128]{2,1,0:T(8,128)} %gather_fusion) | copy-start | bytes 25165828
  93.7 10.6 %copy-start.8 = (f32[64,16,512]{2,1,0:T(8,128)}, f32[64,16,512]{2,1,0:T(8,128)S(1)}, u32[]{:S(2)}) copy-start(f32[64,16,512]{2,1,0:T(8,128)S(1)} %fusion.75) | copy-start | bytes 6291460
  143.5 7.2 collective-permute-start.2
  144.2 6.5 copy-start.9
  144.2 6.5 copy-start.19
  144.3 6.5 collective-permute-start.3
  162.8 10.7 %copy-start.4 = (f32[64,16,512]{2,1,0:T(8,128)}, f32[64,16,512]{2,1,0:T(8,128)S(1)}, u32[]{:S(2)}) copy-start(f32[64,16,512]{2,1,0:T(8,128)S(1)} %fusion.63) | copy-start | bytes 6291460
  206.4 8.2 %copy-start.5 = (f32[64,16,512]{2,1,0:T(8,128)S(1)}, f32[64,16,512]{2,1,0:T(8,128)}, u32[]{:S(2)}) copy-start(f32[64,16,512]{2,1,0:T(8,128)} %copy-done.4) | copy-start | bytes 6291460
  212.6 7.4 collective-permute-start.4
  213.8 6.2 collective-permute-start.5
  232.3 51.4 %copy-start.2 = (f32[64,16,512]{2,1,0:T(8,128)}, f32[64,16,512]{2,1,0:T(8,128)S(1)}, u32[]{:S(2)}) copy-start(f32[64,16,512]{2,1,0:T(8,128)S(1)} %fusion.50) | copy-start | bytes 6291460
  281.8 7.4 collective-permute-start.6
  283.0 6.2 collective-permute-start.7
  352.6 7.3 collective-permute-start.8
  353.7 6.1 collective-permute-start.9
  371.9 10.6 %copy-start.11 = (f32[64,16,512]{2,1,0:T(8,128)}, f32[64,16,512]{2,1,0:T(8,128)S(1)}, u32[]{:S(2)}) copy-start(f32[64,16,512]{2,1,0:T(8,128)S(1)} %fusion.24) | copy-start | bytes 6291460
  421.6 7.2 collective-permute-start.10
  422.8 6.1 collective-permute-start.11
  716.4 52.9 %copy-start.21 = (f32[2,64,1024]{2,1,0:T(8,128)S(1)}, f32[2,64,1024]{2,1,0:T(8,128)}, u32[]{:S(2)}) copy-start(f32[2,64,1024]{2,1,0:T(8,128)} %get-tuple-element.25) | copy-start | bytes 1572868
  728.3 42.3 %copy-start.20 = (f32[2,64,1024]{2,1,0:T(8,128)S(1)}, f32[2,64,1024]{2,1,0:T(8,128)}, u32[]{:S(2)}) copy-start(f32[2,64,1024]{2,1,0:T(8,128)} %get-tuple-element.24) | copy-start | bytes 1572868
  (15 other events, 73.2 us)
Sparse Core Ops, SparseCore 0:
  504.3 129.2 all-reduce.50
where the time goes:
time: 790 us; the launch traced here: 783 us
  matrix products  234 us (30%)
  local copies, waits for them, and re-layouts  203 us (26%)
  waiting for transfers between devices  137 us (17%)
  other arithmetic  123 us (16%)
  blocking collectives  55.2 us (7%)
  between operations  18.9 us (2%)
  starting transfers between devices  11.8 us (1%)
    psum x1, waiting for transfers between devices, local(): gram_matrix = lax.psum(partial_gram, ('band', 'slab'))  128 us
    another operation x15, other arithmetic, local(): factor = jnp.linalg.cholesky(gram_matrix)  79.5 us
    dot_general x6, matrix products, hamiltonian_fn(): jnp.einsum('ajx,anjp->nxp', selector, spread_back, precision=highest)  74.6 us
    dot_general x6, matrix products, hamiltonian_fn(): jnp.einsum('anf,aqf->anq', coupled, atom_tables, precision=highest)  74.1 us
    slice x24, local copies, waits for them, and re-layouts, shifted(): return jnp.concatenate([zeros_part, source[..., :-offset]], axis=-1)  71.5 us
    dot_general x6, matrix products, hamiltonian_fn(): jnp.einsum('anq,aqf->anf', blocks, atom_tables, precision=highest)  56.4 us
    all_to_all x1, blocking collectives, local(): lax.all_to_all(flat_orbitals, 'band', split_axis=1, concat_axis=0, tiled=...  55.2 us
    another operation x4, other arithmetic, local(): return jax.scipy.linalg.solve_triangular(factor, grid_layout, lower=True)  41 us
  transfers between devices with their start and end apart: 13, of which 6 were waited for; matrix products, arithmetic and copies ran while one was open for 11% of the time, Pallas kernels for 0%

commit v1 on v0

--- a/solution.py
+++ b/solution.py
@@ -94,7 +94,9 @@
     grid_layout = lax.all_to_all(flat_orbitals, "band", split_axis=1, concat_axis=0, tiled=True)
     point_total = grid_layout.shape[1] * lax.axis_size(("band", "slab"))
     partial_gram = jnp.dot(grid_layout, grid_layout.T, precision=highest) / point_total
-    gram_matrix = lax.psum(partial_gram, ("band", "slab"))
+    gram_matrix = partial_gram
+    for mesh_axis in ("slab", "band"):
+        gram_matrix = lax.psum(gram_matrix, mesh_axis)
     factor = jnp.linalg.cholesky(gram_matrix)
     return jax.scipy.linalg.solve_triangular(factor, grid_layout, lower=True)
 

time: 790 us -> 778 us (0.985)
  waiting for transfers between devices: 137 us -> 124 us
    psum x1 -> x2, waiting for transfers between devices: 128 us -> 116 us  [local(): gram_matrix = lax.psum(gram_matrix, mesh_axis)]
  transfers between devices with their start and end apart: 13 -> 14, of which waited for: 6 -> 7; matrix products, arithmetic and copies ran while one was open for 11% -> 11% of each run, Pallas kernels for 0% -> 0%
where the time goes in v1:
time: 778 us; the launch traced here: 770 us
  matrix products  234 us (30%)
  local copies, waits for them, and re-layouts  203 us (26%)
  waiting for transfers between devices  124 us (16%)
  other arithmetic  123 us (16%)
  blocking collectives  55.2 us (7%)
  between operations  18.9 us (2%)
  starting transfers between devices  12 us (2%)
    psum x2, waiting for transfers between devices, local(): gram_matrix = lax.psum(gram_matrix, mesh_axis)  116 us
    another operation x15, other arithmetic, local(): factor = jnp.linalg.cholesky(gram_matrix)  79.6 us
    dot_general x6, matrix products, hamiltonian_fn(): jnp.einsum('ajx,anjp->nxp', selector, spread_back, precision=highest)  75 us
    dot_general x6, matrix products, hamiltonian_fn(): jnp.einsum('anf,aqf->anq', coupled, atom_tables, precision=highest)  74.1 us
    slice x24, local copies, waits for them, and re-layouts, shifted(): return jnp.concatenate([zeros_part, source[..., :-offset]], axis=-1)  71.5 us
    dot_general x6, matrix products, hamiltonian_fn(): jnp.einsum('anq,aqf->anf', blocks, atom_tables, precision=highest)  56.2 us
    all_to_all x1, blocking collectives, local(): lax.all_to_all(flat_orbitals, 'band', split_axis=1, concat_axis=0, tiled=...  55.2 us
    another operation x4, other arithmetic, local(): return jax.scipy.linalg.solve_triangular(factor, grid_layout, lower=True)  41 us
  transfers between devices with their start and end apart: 14, of which 7 were waited for; matrix products, arithmetic and copies ran while one was open for 11% of the time, Pallas kernels for 0%

profile of v1, /device:TPU:0, one launch (start us, length us, event | category | flops | bytes accessed | tf_op | source)
XLA Modules:
  0.0 770.5 jit_solution(2498419455078202497)
XLA Ops:
  51.0 10.4 %convolution_multiply_fusion.6 = f32[8,64,128]{2,1,0:T(8,128)S(1)} fusion(f32[8,64,2048]{2,1,0:T(8,128)} %reshape.122, f32[8,128]{1,0:T(8,128)S(1)} %copy-done.24, f32[8,2048,128]{2,1,0:T(8,128)} %gather_fusion, pred[8]{0:T(512)(128)(4,1)S(1)} %compare_and_fusion), kind=kOutput, calls=%fused_computation.154 | convolution fusion | flops 1612775424 | bytes 12849160 | tf_op jit(solution)/shard_map/anq,aqf->anf/dot_general | solution.py:71
  61.5 10.5 %fusion.153 = f32[8,64,2048]{2,1,0:T(8,128)} fusion(f32[8,64,128]{2,1,0:T(8,128)S(1)} %convolution_multiply_fusion.6, f32[8,2048,128]{2,1,0:T(8,128)S(1)} %copy-done, pred[8]{0:T(512)(128)(4,1)S(1)} %compare_and_fusion), kind=kOutput, calls=%fused_computation.243 | convolution fusion | flops 1612709888 | bytes 12845064 | tf_op jit(solution)/shard_map/anf,aqf->anq/dot_general | solution.py:72
  81.7 12.0 %fusion.75 = f32[64,16,512]{2,1,0:T(8,128)S(1)} fusion(f32[64,2,512]{2,1,0:T(2,128)S(1)} %collective-permute-done, f32[64,16,512]{2,1,0:T(8,128)S(1)} %copy-done.1, f32[64,18,512]{2,1,0:T(8,128)} %copy-done.23, f32[64,16,510]{2,1,0:T(8,128)} %get-tuple-element.84, f32[64,16,448]{2,1,0:T(8,128)} %get-tuple-element.82, ...), kind=kOutput, calls=%fused_computation.107 | convolution fusion | flops 221249536 | bytes 28846600 | tf_op jit(solution)/shard_map/ajx,anjp->nxp/dot_general | solution.py:74
  124.7 12.7 %fusion.152 = f32[8,64,2048]{2,1,0:T(8,128)} fusion(f32[8,64,128]{2,1,0:T(8,128)S(1)} %convolution_multiply_fusion.5, f32[8,2048,128]{2,1,0:T(8,128)} %gather_fusion, pred[8]{0:T(512)(128)(4,1)S(1)} %compare_and_fusion), kind=kOutput, calls=%fused_computation.242 | convolution fusion | flops 1612709888 | bytes 12845064 | tf_op jit(solution)/shard_map/anf,aqf->anq/dot_general | solution.py:72
  150.8 12.0 %fusion.63 = f32[64,16,512]{2,1,0:T(8,128)S(1)} fusion(f32[64,16,512]{2,1,0:T(8,128)S(1)} %copy-done.9, f32[64,2,512]{2,1,0:T(2,128)S(1)} %collective-permute-done.3, f32[64,2,512]{2,1,0:T(2,128)S(1)} %collective-permute-done.2, f32[64,16,512]{2,1,0:T(8,128)S(1)} %copy-done.1, f32[64,16,510]{2,1,0:T(8,128)} %get-tuple-element.74, ...), kind=kOutput, calls=%fused_computation.95 | convolution fusion | flops 223346688 | bytes 27011596 | tf_op jit(solution)/shard_map/ajx,anjp->nxp/dot_general | solution.py:74
  193.7 12.7 %fusion.151 = f32[8,64,2048]{2,1,0:T(8,128)} fusion(f32[8,64,128]{2,1,0:T(8,128)S(1)} %convolution_multiply_fusion.4, f32[8,2048,128]{2,1,0:T(8,128)} %gather_fusion, pred[8]{0:T(512)(128)(4,1)S(1)} %compare_and_fusion), kind=kOutput, calls=%fused_computation.241 | convolution fusion | flops 1612709888 | bytes 12845064 | tf_op jit(solution)/shard_map/anf,aqf->anq/dot_general | solution.py:72
  220.0 12.3 %fusion.50 = f32[64,16,512]{2,1,0:T(8,128)S(1)} fusion(f32[64,16,512]{2,1,0:T(8,128)S(1)} %copy-done.6, f32[64,2,512]{2,1,0:T(2,128)S(1)} %collective-permute-done.5, f32[64,2,512]{2,1,0:T(2,128)S(1)} %collective-permute-done.4, f32[64,16,512]{2,1,0:T(8,128)S(1)} %copy-done.10, f32[64,16,510]{2,1,0:T(8,128)} %get-tuple-element.64, ...), kind=kOutput, calls=%fused_computation.82 | convolution fusion | flops 223346688 | bytes 27011596 | tf_op jit(solution)/shard_map/ajx,anjp->nxp/dot_general | solution.py:74
  263.0 12.7 %fusion.150 = f32[8,64,2048]{2,1,0:T(8,128)} fusion(f32[8,64,128]{2,1,0:T(8,128)S(1)} %convolution_multiply_fusion.3, f32[8,2048,128]{2,1,0:T(8,128)} %gather_fusion, pred[8]{0:T(512)(128)(4,1)S(1)} %compare_and_fusion), kind=kOutput, calls=%fused_computation.240 | convolution fusion | flops 1612709888 | bytes 12845064 | tf_op jit(solution)/shard_map/anf,aqf->anq/dot_general | solution.py:72
  289.2 13.8 %fusion.37 = f32[64,16,512]{2,1,0:T(8,128)S(1)} fusion(f32[64,16,512]{2,1,0:T(8,128)} %copy-done.2, f32[64,2,512]{2,1,0:T(2,128)S(1)} %collective-permute-done.7, f32[64,2,512]{2,1,0:T(2,128)S(1)} %collective-permute-done.6, f32[64,16,512]{2,1,0:T(8,128)S(1)} %copy-done.7, f32[64,16,510]{2,1,0:T(8,128)} %get-tuple-element.54, ...), kind=kOutput, calls=%fused_computation.69 | convolution fusion | flops 223346688 | bytes 27011596 | tf_op jit(solution)/shard_map/ajx,anjp->nxp/dot_general | solution.py:74
  333.8 12.7 %fusion.149 = f32[8,64,2048]{2,1,0:T(8,128)} fusion(f32[8,64,128]{2,1,0:T(8,128)S(1)} %convolution_multiply_fusion.2, f32[8,2048,128]{2,1,0:T(8,128)} %gather_fusion, pred[8]{0:T(512)(128)(4,1)S(1)} %compare_and_fusion), kind=kOutput, calls=%fused_computation.239 | convolution fusion | flops 1612709888 | bytes 12845064 | tf_op jit(solution)/shard_map/anf,aqf->anq/dot_general | solution.py:72
  359.9 12.0 %fusion.24 = f32[64,16,512]{2,1,0:T(8,128)S(1)} fusion(f32[64,16,512]{2,1,0:T(8,128)S(1)} %fusion.37, f32[64,2,512]{2,1,0:T(2,128)S(1)} %collective-permute-done.9, f32[64,2,512]{2,1,0:T(2,128)S(1)} %collective-permute-done.8, f32[64,16,512]{2,1,0:T(8,128)S(1)} %copy-done.3, f32[64,16,510]{2,1,0:T(8,128)} %get-tuple-element.44, ...), kind=kOutput, calls=%fused_computation.56 | convolution fusion | flops 223346688 | bytes 27011596 | tf_op jit(solution)/shard_map/ajx,anjp->nxp/dot_general | solution.py:74
  402.6 12.8 %fusion.148 = f32[8,64,2048]{2,1,0:T(8,128)} fusion(f32[8,64,128]{2,1,0:T(8,128)S(1)} %convolution_multiply_fusion.1, f32[8,2048,128]{2,1,0:T(8,128)} %gather_fusion, pred[8]{0:T(512)(128)(4,1)S(1)} %compare_and_fusion), kind=kOutput, calls=%fused_computation.238 | convolution fusion | flops 1612709888 | bytes 12845064 | tf_op jit(solution)/shard_map/anf,aqf->anq/dot_general | solution.py:72
  428.6 12.9 %fusion.11 = f32[64,16,512]{2,1,0:T(8,128)} fusion(f32[64,16,512]{2,1,0:T(8,128)S(1)} %copy-done.12, f32[64,2,512]{2,1,0:T(2,128)S(1)} %collective-permute-done.11, f32[64,2,512]{2,1,0:T(2,128)S(1)} %collective-permute-done.10, f32[64,16,512]{2,1,0:T(8,128)S(1)} %fusion.37, f32[64,16,510]{2,1,0:T(8,128)} %get-tuple-element.34, ...), kind=kOutput, calls=%fused_computation.43 | convolution fusion | flops 223346688 | bytes 27011596 | tf_op jit(solution)/shard_map/ajx,anjp->nxp/dot_general | solution.py:74
  444.7 55.2 %all_to_all.19 = f32[64,8,1024]{2,0,1:T(8,128)S(1)} all-to-all(f32[64,8,1024]{2,0,1:T(8,128)S(1)} %copy.29), channel_id=1, replica_groups=mesh['band'=8,'slab'=4] {'band'}, dimensions={1} | all-to-all | bytes 4194304 | tf_op jit(solution)/shard_map/all_to_all | solution.py:94
  504.6 34.8 %all-reduce.52.cloned.1.call-done = f32[512,512]{0,1:T(8,128)} async-done(((f32[512,512]{0,1:T(8,128)}), f32[512,512]{0,1:T(8,128)}) %all-reduce.52.cloned.1.call-update) | async-done | bytes 1048592 | tf_op jit(solution)/shard_map/psum | solution.py:99
  540.8 80.9 %all-reduce.54.cloned.1.call-done = f32[512,512]{0,1:T(8,128)} async-done(((f32[512,512]{0,1:T(8,128)}), f32[512,512]{0,1:T(8,128)}) %all-reduce.54.cloned.1.call-update) | async-done | bytes 1048592 | tf_op jit(solution)/shard_map/psum | solution.py:99
  623.6 11.7 %cholesky.104 = f32[128,128]{1,0:T(8,128)S(1)} custom-call(f32[128,128]{1,0:T(8,128)S(1)} %cholesky.266), custom_call_target="Cholesky" | custom-call | tf_op jit(solution)/shard_map/jit(cholesky)/cholesky | solution.py:100
  635.5 9.8 %custom-call.31 = f32[1,128,128]{1,2,0:T(8,128)S(1)} custom-call(f32[1,128,128]{2,1,0:T(8,128)S(1)} %get-tuple-element.96), custom_call_target="InvertDiagBlocksLowerTriangular" | custom-call | tf_op jit(solution)/shard_map/jit(cholesky)/cholesky | solution.py:100
  646.0 11.7 %cholesky.217 = f32[128,128]{1,0:T(8,128)S(1)} custom-call(f32[128,128]{1,0:T(8,128)S(1)} %cholesky.270), custom_call_target="Cholesky" | custom-call | tf_op jit(solution)/shard_map/jit(cholesky)/cholesky | solution.py:100
  659.1 10.0 %custom-call.32 = f32[1,128,128]{1,2,0:T(8,128)S(1)} custom-call(f32[1,128,128]{2,1,0:T(8,128)S(1)} %get-tuple-element.93), custom_call_target="InvertDiagBlocksLowerTriangular" | custom-call | tf_op jit(solution)/shard_map/jit(cholesky)/cholesky | solution.py:100
  669.7 11.7 %cholesky.238 = f32[128,128]{1,0:T(8,128)S(1)} custom-call(f32[128,128]{1,0:T(8,128)S(1)} %cholesky.275), custom_call_target="Cholesky" | custom-call | tf_op jit(solution)/shard_map/jit(cholesky)/cholesky | solution.py:100
  682.2 9.8 %custom-call.33 = f32[1,128,128]{1,2,0:T(8,128)S(1)} custom-call(f32[1,128,128]{2,1,0:T(8,128)S(1)} %get-tuple-element.90), custom_call_target="InvertDiagBlocksLowerTriangular" | custom-call | tf_op jit(solution)/shard_map/jit(cholesky)/cholesky | solution.py:100
  692.6 11.9 %cholesky.255 = f32[128,128]{1,0:T(8,128)S(1)} custom-call(f32[128,128]{1,0:T(8,128)S(1)} %convolution_subtract_fusion.4), custom_call_target="Cholesky" | custom-call | tf_op jit(solution)/shard_map/jit(cholesky)/cholesky | solution.py:100
  716.2 39.3 %custom-call.34 = f32[4,128,128]{1,2,0:T(8,128)S(1)} custom-call(f32[4,128,128]{2,1,0:T(8,128)S(1)} %get-tuple-element.12), custom_call_target="InvertDiagBlocksLowerTriangular" | custom-call | tf_op jit(solution)/shard_map/jit(_solve_triangular)/triangular_solve | solution.py:101
  (199 shorter events, 313.3 us)
Async XLA Ops:
  6.5 532.9 %all-reduce.52.cloned.1.call-start = ((), (), s32[]{:S(2)}) async-start(), calls=%async_computation.1 | async-start | bytes 2097152 | tf_op jit(solution)/shard_map/psum | solution.py:99
  8.3 70.2 %collective-permute-start.1 = (f32[64,2,512]{2,1,0:T(2,128)S(1)}, f32[64,2,512]{2,1,0:T(2,128)S(1)}, u32[]{:S(2)}, u32[]{:S(2)}) collective-permute-start(f32[64,2,512]{2,1,0:T(2,128)S(1)} %get-tuple-element.85), channel_id=1, source_target_pairs={{1,0},{2,1},{3,2},{0,3},{5,4},{6,5},{7,6},{4,7},{9,8},{10,9},{11,1... | collective-permute-start | bytes 786440 | tf_op jit(solution)/shard_map/ppermute | solution.py:23
  10.8 67.9 %collective-permute-start = (f32[64,2,512]{2,1,0:T(2,128)S(1)}, f32[64,2,512]{2,1,0:T(2,128)S(1)}, u32[]{:S(2)}, u32[]{:S(2)}) collective-permute-start(f32[64,2,512]{2,1,0:T(2,128)S(1)} %get-tuple-element.86), channel_id=1, source_target_pairs={{0,1},{1,2},{2,3},{3,0},{4,5},{5,6},{6,7},{7,4},{8,9},{9,10},{10,1... | collective-permute-start | bytes 786440 | tf_op jit(solution)/shard_map/ppermute | solution.py:22
  44.4 6.6 copy-start.24
  51.0 10.4 %copy-start = (f32[8,2048,128]{2,1,0:T(8,128)S(1)}, f32[8,2048,128]{2,1,0:T(8,128)}, u32[]{:S(2)}) copy-start(f32[8,2048,128]{2,1,0:T(8,128)} %gather_fusion) | copy-start | bytes 25165828
  93.7 10.6 %copy-start.8 = (f32[64,16,512]{2,1,0:T(8,128)}, f32[64,16,512]{2,1,0:T(8,128)S(1)}, u32[]{:S(2)}) copy-start(f32[64,16,512]{2,1,0:T(8,128)S(1)} %fusion.75) | copy-start | bytes 6291460
  143.5 7.2 collective-permute-start.2
  144.2 6.5 copy-start.19
  144.3 6.5 collective-permute-start.3
  162.8 10.7 %copy-start.4 = (f32[64,16,512]{2,1,0:T(8,128)}, f32[64,16,512]{2,1,0:T(8,128)S(1)}, u32[]{:S(2)}) copy-start(f32[64,16,512]{2,1,0:T(8,128)S(1)} %fusion.63) | copy-start | bytes 6291460
  206.4 8.2 %copy-start.5 = (f32[64,16,512]{2,1,0:T(8,128)S(1)}, f32[64,16,512]{2,1,0:T(8,128)}, u32[]{:S(2)}) copy-start(f32[64,16,512]{2,1,0:T(8,128)} %copy-done.4) | copy-start | bytes 6291460
  212.6 7.4 collective-permute-start.4
  213.8 6.2 collective-permute-start.5
  232.3 51.4 %copy-start.2 = (f32[64,16,512]{2,1,0:T(8,128)}, f32[64,16,512]{2,1,0:T(8,128)S(1)}, u32[]{:S(2)}) copy-start(f32[64,16,512]{2,1,0:T(8,128)S(1)} %fusion.50) | copy-start | bytes 6291460
  281.8 7.4 collective-permute-start.6
  283.0 6.2 collective-permute-start.7
  352.6 7.3 collective-permute-start.8
  353.7 6.1 collective-permute-start.9
  371.8 10.6 %copy-start.11 = (f32[64,16,512]{2,1,0:T(8,128)}, f32[64,16,512]{2,1,0:T(8,128)S(1)}, u32[]{:S(2)}) copy-start(f32[64,16,512]{2,1,0:T(8,128)S(1)} %fusion.24) | copy-start | bytes 6291460
  421.4 7.2 collective-permute-start.10
  422.6 6.1 collective-permute-start.11
  504.4 117.3 %all-reduce.54.cloned.1.call-start = ((), (), s32[]{:S(2)}) async-start(), calls=%async_computation.2 | async-start | bytes 2097152 | tf_op jit(solution)/shard_map/psum | solution.py:99
  704.5 52.7 %copy-start.21 = (f32[2,64,1024]{2,1,0:T(8,128)S(1)}, f32[2,64,1024]{2,1,0:T(8,128)}, u32[]{:S(2)}) copy-start(f32[2,64,1024]{2,1,0:T(8,128)} %get-tuple-element.25) | copy-start | bytes 1572868
  716.2 42.3 %copy-start.20 = (f32[2,64,1024]{2,1,0:T(8,128)S(1)}, f32[2,64,1024]{2,1,0:T(8,128)}, u32[]{:S(2)}) copy-start(f32[2,64,1024]{2,1,0:T(8,128)} %get-tuple-element.24) | copy-start | bytes 1572868
  (16 other events, 79.6 us)
Sparse Core Ops, SparseCore 0:
  504.5 34.8 all-reduce.51
  542.9 78.7 all-reduce.53
